TPU v7x, 32 devices: a whole 2x2x4 slice. The times are simulated.
32 devices in a mesh: pipe: 4 (over y, x), dp: 8 (over z, core).
Axes of the slice: x: 2, y: 2, z: 4, core: 2. Of those that a mesh axis runs over, the one named last changes fastest.
Arguments:
- acts: bfloat16 [4, 2048, 3072], P('pipe', 'dp'), may hold values from -24 to 24, as said below
- grad: float32 [12288, 4096], P('pipe', 'dp'), may hold values from -6 to 6
- owner_of: int32 [4, 12], replicated, may hold values from 0 to 3, as said below
Outputs:
- precond: float32 [12288, 4096], P('pipe', 'dp')
- held_inverse: float32 [4, 24, 256, 256], P('pipe', None, 'dp')
Inputs may be any that keep to these rules, and one draw needn't show every extreme that they name: `acts`: column and token scales of the activations vary; entries lie within the range. `owner_of`: no section index owns more than 24 blocks in all, and some section index owns exactly 24.
All inputs are finite; a program needn't handle non-finite values.
Results may differ from a plain program's by a relative error of at most 0.0003.
Values sent between devices are 32-bit elements; how exact they have to be, the bound alone decides.
A program may use at most 128 MiB of HBM per device.

v0:
```python
import jax
import jax.numpy as jnp
from jax import lax
from jax.sharding import PartitionSpec as P

BLK = 256
HOST = 24
damping_ratio = 0.1


def invert_blocks(factor, vacant):
    order_size = factor.shape[-1]
    diagonal_sum = jnp.sum(jnp.diagonal(factor, axis1=1, axis2=2), axis=1)
    damping = damping_ratio * diagonal_sum / order_size
    identity = jnp.eye(order_size, dtype=factor.dtype)
    shifted = factor + (damping + vacant)[:, None, None] * identity
    cholesky_lower = jnp.linalg.cholesky(shifted)
    identity_stack = jnp.broadcast_to(identity, factor.shape)
    inv_lower = lax.linalg.triangular_solve(
        cholesky_lower, identity_stack, left_side=True, lower=True
    )
    return jnp.einsum("mkr,mkc->mrc", inv_lower, inv_lower, precision=lax.Precision.HIGHEST)


def slot_tables(owner_of):
    owners_flat = owner_of.reshape(-1)
    positions = jnp.arange(owners_flat.shape[0], dtype=jnp.int32)
    matches = owners_flat[:, None] == owners_flat[None, :]
    before = positions[None, :] < positions[:, None]
    slot_rank = jnp.sum((matches & before).astype(jnp.int32), axis=1)
    return (owners_flat, slot_rank)


def shards(acts, grad, owner_of):
    tokens = acts.shape[1]
    feature_count = acts.shape[2]
    nblocks = feature_count // BLK
    data_count = lax.axis_size("dp")
    section_count = lax.axis_size("pipe")
    row_share = BLK // data_count
    all_tokens = tokens * data_count
    section_index = lax.axis_index("pipe")
    member = lax.axis_index("dp")
    features = acts[0].reshape(tokens, nblocks, BLK)
    owners_flat, slot_rank = slot_tables(owner_of)
    slot_ids = jnp.arange(HOST, dtype=jnp.int32)
    pick_mine = (
        (owners_flat[None, :] == section_index) & (slot_rank[None, :] == slot_ids[:, None])
    ).astype(jnp.float32)
    own_owners = lax.dynamic_index_in_dim(owner_of, section_index, 0, keepdims=False)
    own_ranks = lax.dynamic_index_in_dim(
        slot_rank.reshape(section_count, nblocks), section_index, 0, keepdims=False
    )
    target = own_owners * HOST + own_ranks
    pick_back = (
        jnp.arange(section_count * HOST, dtype=jnp.int32)[None, :] == target[:, None]
    ).astype(jnp.float32)
    block_terms = jnp.einsum("tbr,tbc->rbc", features, features, preferred_element_type=jnp.float32)
    my_rows = lax.psum_scatter(
        block_terms.reshape(row_share * lax.axis_size("dp"), nblocks * BLK),
        "dp",
        scatter_dimension=0,
        tiled=True,
    )
    pieces = lax.all_gather(my_rows, "pipe", axis=0, tiled=True).reshape(
        section_count, row_share, nblocks, BLK
    )
    hosted = jnp.einsum(
        "jsb,srbc->jrc",
        pick_mine.reshape(HOST, section_count, nblocks),
        pieces,
        precision=lax.Precision.HIGHEST,
    )
    occupied = jnp.sum(pick_mine, axis=1)
    per_member = (HOST + data_count - 1) // data_count
    padded_count = per_member * data_count
    padded = jnp.pad(hosted, ((0, padded_count - HOST), (0, 0), (0, 0)))
    mine_blocks = lax.all_to_all(padded, "dp", split_axis=0, concat_axis=1, tiled=True) / all_tokens
    padded_flags = jnp.pad(occupied, (0, padded_count - HOST))
    held_flags = lax.dynamic_slice_in_dim(padded_flags, member * per_member, per_member, 0)
    inverted = invert_blocks(mine_blocks, 1.0 - held_flags) * held_flags[:, None, None]
    spread_rows = lax.all_to_all(inverted, "dp", split_axis=1, concat_axis=0, tiled=True)
    held_rows = spread_rows[:HOST]
    returned = lax.all_gather(held_rows, "pipe", axis=0, tiled=True)
    own_rows = jnp.einsum("bm,mrc->brc", pick_back, returned, precision=lax.Precision.HIGHEST)
    inverse = lax.all_gather(own_rows, "dp", axis=1, tiled=True)
    grad_blocks = grad.reshape(nblocks, BLK, grad.shape[1])
    precond = jnp.einsum("brk,bkc->brc", inverse, grad_blocks, precision=lax.Precision.HIGHEST)
    return (precond.reshape(feature_count, grad.shape[1]), held_rows[None])


def solution(mesh):
    placed = (P("pipe", "dp", None), P("pipe", "dp"), P())
    return jax.shard_map(
        shards,
        mesh=mesh,
        in_specs=placed,
        out_specs=(P("pipe", "dp"), P("pipe", None, "dp", None)),
        check_vma=False,
    )
```

profile of v0, /device:TPU:0, one launch (start us, length us, event | category | flops | bytes accessed | tf_op | source)
XLA Modules:
  0.0 447.4 jit_solution(14781126711529102693)
XLA Ops:
  7.2 1.7 copy.123
  8.9 2.3 fusion.30
  11.2 3.5 copy.125
  14.8 43.2 %reduce-scatter.2.cloned.1.call-done = f32[32,3072]{1,0:T(8,128)} async-done(((f32[256,3072]{1,0:T(8,128)}), f32[32,3072]{1,0:T(8,128)}) %reduce-scatter.2.cloned.1.call-update) | async-done | bytes 393232 | tf_op jit(solution)/shard_map/reduce_scatter | solution.py:59
  58.4 31.6 %all-gather.4.cloned.1.call-done = f32[128,3072]{1,0:T(8,128)} async-done(((f32[32,3072]{1,0:T(8,128)}), f32[128,3072]{1,0:T(8,128)}) %all-gather.4.cloned.1.call-update) | async-done | bytes 1572880 | tf_op jit(solution)/shard_map/all_gather | solution.py:65
  90.0 1.7 reshape.95
  91.7 0.9 convolution_bitcast_fusion
  92.6 1.1 copy.127
  93.7 4.6 %all-to-all-start = ((f32[24,32,256]{2,1,0:T(8,128)}), f32[24,32,256]{2,1,0:T(8,128)S(1)}, u32[]{:S(2)}, u32[]{:S(2)}) async-start(f32[24,32,256]{2,1,0:T(8,128)} %copy.127), calls=%async_computation.1 | async-start | bytes 1572864 | tf_op jit(solution)/shard_map/all_to_all | solution.py:78
  98.3 0.2 all-gather.6.cloned.1.call-start
  98.6 0.7 copy.135
  99.5 0.5 iota_multiply_fusion
  100.1 0.6 iota_compare_fusion.2
  100.8 0.6 iota_compare_fusion.1
  101.4 17.8 %all-to-all-done = f32[24,32,256]{2,1,0:T(8,128)S(1)} async-done(((f32[24,32,256]{2,1,0:T(8,128)}), f32[24,32,256]{2,1,0:T(8,128)S(1)}, u32[]{:S(2)}, u32[]{:S(2)}) %all-to-all-start) | async-done | bytes 786464 | tf_op jit(solution)/shard_map/all_to_all | solution.py:78
  119.4 16.8 %copy.129 = f32[3,256,256]{0,2,1:T(8,128)} copy(f32[3,256,256]{2,1,0:T(8,128)S(1)} %bitcast.75) | data formatting | bytes 1572864 | tf_op jit(solution)/shard_map/div | solution.py:78
  136.2 0.3 copy.130
  136.5 2.3 gather_fusion
  138.9 0.6 subtract_add_fusion
  139.4 0.5 copy-done.4
  140.1 0.3 copy.131
  140.4 0.8 fusion.5
  141.3 35.2 %custom-call.16 = f32[3,128,128]{2,1,0:T(8,128)S(1)} custom-call(f32[3,128,128]{2,1,0:T(8,128)S(1)} %cholesky.122), custom_call_target="Cholesky" | custom-call | tf_op jit(solution)/shard_map/jit(cholesky)/cholesky | solution.py:17
  176.5 0.8 select_bitcast_fusion
  177.3 29.5 %custom-call.17 = f32[3,1,128,128]{2,3,1,0:T(8,128)S(1)} custom-call(f32[3,1,128,128]{3,2,1,0:T(8,128)S(1)} %select_bitcast_fusion), custom_call_target="InvertDiagBlocksLowerTriangular" | custom-call | tf_op jit(solution)/shard_map/jit(cholesky)/cholesky | solution.py:17
  206.8 0.4 constant_dynamic-update-slice_fusion.1
  207.1 0.5 convolution_subtract_fusion.1
  207.7 35.4 %custom-call.18 = f32[3,128,128]{2,1,0:T(8,128)S(1)} custom-call(f32[3,128,128]{2,1,0:T(8,128)S(1)} %convolution_subtract_fusion.1), custom_call_target="Cholesky" | custom-call | tf_op jit(solution)/shard_map/jit(cholesky)/cholesky | solution.py:17
  243.6 5.4 %while.1 = (s32[]{:T(128)}, f32[3,256,256]{2,1,0:T(8,128)S(1)}, s32[2,2]{1,0:T(2,128)S(1)}, f32[2,3,128,128]{3,2,0,1:T(8,128)}, s32[]{:T(128)}) while((s32[]{:T(128)}, f32[3,256,256]{2,1,0:T(8,128)S(1)}, s32[2,2]{1,0:T(2,128)S(1)}, f32[2,3,128,128]{3,2,0,1:T(8,128)}, s32[]{:T(128)}) %tuple.29), condition=%wide.while_cond, body=%wide.while_body.sunk | while | flops 2 | bytes 394849 | solution.py:19
  243.6 0.6 fusion.42
  244.2 2.1 bitcast_dynamic-update-slice_fusion.2
  246.2 0.6 fusion.42
  246.9 2.1 bitcast_dynamic-update-slice_fusion.2
  248.9 59.8 %custom-call.19 = f32[3,2,128,128]{2,3,1,0:T(8,128)S(1)} custom-call(f32[3,2,128,128]{3,2,1,0:T(8,128)} %bitcast.83), custom_call_target="InvertDiagBlocksLowerTriangular" | custom-call | tf_op jit(solution)/shard_map/triangular_solve | solution.py:19
  308.7 0.5 fusion.9
  309.2 0.5 convolution_subtract_fusion
  309.7 0.5 fusion.8
  310.3 1.4 convolution_multiply_fusion
  311.7 0.5 copy.140
  312.3 29.0 %all_to_all.27 = f32[3,256,256]{2,0,1:T(4,128)S(1)} all-to-all(f32[3,256,256]{2,0,1:T(4,128)S(1)} %copy.140), channel_id=1, replica_groups=mesh['pipe'=4,'dp'=8] {'dp'}, dimensions={1} | all-to-all | bytes 1572864 | tf_op jit(solution)/shard_map/all_to_all | solution.py:82
  341.4 1.0 copy.142
  342.4 0.3 all-gather.8.cloned.1.call-start
  342.7 0.7 fusion.26
  343.4 40.9 %all-gather.6.cloned.1.call-done = f32[96,32,256]{2,1,0:T(8,128)} async-done(((f32[24,32,256]{2,1,0:T(8,128)}), f32[96,32,256]{2,1,0:T(8,128)}) %all-gather.6.cloned.1.call-update) | async-done | bytes 3145744 | tf_op jit(solution)/shard_map/all_gather | solution.py:84
  384.4 4.7 %fusion = f32[12,32,256]{2,0,1:T(8,128)S(1)} fusion(f32[96,32,256]{2,1,0:T(8,128)} %all-gather.6.cloned.1.call-done, s32[12]{0:T(128)S(1)} %fusion.26), kind=kOutput, calls=%fused_computation.3 | convolution fusion | flops 113247360 | bytes 3538992 | tf_op jit(solution)/shard_map/bm,mrc->brc/dot_general | solution.py:85
  389.0 1.0 copy.144
  390.0 38.4 %all-gather.8.cloned.1.call-done = f32[12,256,256]{2,1,0:T(8,128)} async-done(((f32[12,32,256]{2,1,0:T(8,128)}), f32[12,256,256]{2,1,0:T(8,128)}) %all-gather.8.cloned.1.call-update) | async-done | bytes 3145744 | tf_op jit(solution)/shard_map/all_gather | solution.py:86
  428.4 12.5 %fusion.31 = f32[12,256,512]{2,1,0:T(8,128)} fusion(f32[12,256,256]{2,1,0:T(8,128)} %all-gather.8.cloned.1.call-done, f32[12,256,512]{2,1,0:T(8,128)} %bitcast.77), kind=kOutput, calls=%fused_computation.66 | convolution fusion | flops 4831838208 | bytes 15728640 | tf_op jit(solution)/shard_map/brk,bkc->brc/dot_general | solution.py:88
  (45 shorter events, 1.8 us)
Async XLA Ops:
  7.2 50.8 %reduce-scatter.2.cloned.1.call-start = ((), (), s32[]{:S(2)}) async-start(), calls=%async_computation.3 | async-start | bytes 3538944 | tf_op jit(solution)/shard_map/reduce_scatter | solution.py:59
  14.7 43.3 %copy-start.2 = (s32[4,12]{1,0:T(4,128)S(1)}, s32[4,12]{1,0:T(4,128)}, u32[]{:S(2)}) copy-start(s32[4,12]{1,0:T(4,128)} %param.5) | copy-start | bytes 580
  14.7 75.2 %all-gather.4.cloned.1.call-start = ((), (), s32[]{:S(2)}) async-start(), calls=%async_computation.4 | async-start | bytes 1966080 | tf_op jit(solution)/shard_map/all_gather | solution.py:65
  58.4 34.2 %copy-start.3 = (s32[4,12]{1,0:T(4,128)}, s32[4,12]{1,0:T(4,128)S(1)}, u32[]{:S(2)}) copy-start(s32[4,12]{1,0:T(4,128)S(1)} %reshape.93) | copy-start | bytes 580
  93.7 25.6 %all-to-all-start = ((f32[24,32,256]{2,1,0:T(8,128)}), f32[24,32,256]{2,1,0:T(8,128)S(1)}, u32[]{:S(2)}, u32[]{:S(2)}) async-start(f32[24,32,256]{2,1,0:T(8,128)} %copy.127), calls=%async_computation.1 | async-start | bytes 1572864 | tf_op jit(solution)/shard_map/all_to_all | solution.py:78
  98.3 286.0 %all-gather.6.cloned.1.call-start = ((), (), s32[]{:S(2)}) async-start(), calls=%async_computation.5 | async-start | bytes 3932160 | tf_op jit(solution)/shard_map/all_gather | solution.py:84
  139.4 0.5 copy-start.4
  140.4 102.9 %copy-start.1 = (pred[256,256]{1,0:T(8,128)(4,1)S(1)}, pred[256,256]{1,0:T(8,128)(4,1)}, u32[]{:S(2)}) copy-start(pred[256,256]{1,0:T(8,128)(4,1)} %iota_compare_fusion.1) | copy-start | bytes 196612
  141.2 102.3 %copy-start.6 = (s32[2]{0:T(128)S(1)}, s32[2]{0:T(128)}, u32[]{:S(2)}) copy-start(s32[2]{0:T(128)} %iota_multiply_fusion) | copy-start | bytes 28
  176.5 132.2 %copy-start = (f32[128,256]{1,0:T(8,128)S(1)}, f32[128,256]{1,0:T(8,128)}, u32[]{:S(2)}) copy-start(f32[128,256]{1,0:T(8,128)} %copy.135) | copy-start | bytes 393220
  243.3 67.0 %copy-start.5 = (f32[3]{0:T(128)S(1)}, f32[3]{0:T(128)}, u32[]{:S(2)}) copy-start(f32[3]{0:T(128)} %get-tuple-element.21) | copy-start | bytes 40
  342.4 86.0 %all-gather.8.cloned.1.call-start = ((), (), s32[]{:S(2)}) async-start(), calls=%async_computation.6 | async-start | bytes 3538944 | tf_op jit(solution)/shard_map/all_gather | solution.py:86
Sparse Core Ops, SparseCore 0:
  14.9 43.0 reduce-scatter.1
  59.8 30.0 all-gather.3
  342.5 41.7 all-gather.5
  390.1 38.1 all-gather.7
where the time goes:
time: 448 us; the launch traced here: 447 us
  waiting for transfers between devices  172 us (38%)
  other arithmetic  165 us (37%)
  local copies, waits for them, and re-layouts  37.5 us (8%)
  blocking collectives  29 us (6%)
  matrix products  24.2 us (5%)
  between operations  14.1 us (3%)
  starting transfers between devices  5.21 us (1%)
    another operation x9, other arithmetic, invert_blocks(): cholesky_lower = jnp.linalg.cholesky(shifted)  102 us
    another operation x4, other arithmetic, invert_blocks(): lax.linalg.triangular_solve(cholesky_lower, identity_stack, left_side=Tru...  61.1 us
    reduce_scatter x1, waiting for transfers between devices, shards(): lax.psum_scatter(block_terms.reshape(row_share * lax.axis_size('dp'), nbl...  43.2 us
    all_gather x1, waiting for transfers between devices, shards(): returned = lax.all_gather(held_rows, 'pipe', axis=0, tiled=True)  40.9 us
    all_gather x1, waiting for transfers between devices, shards(): inverse = lax.all_gather(own_rows, 'dp', axis=1, tiled=True)  38.4 us
    all_gather x1, waiting for transfers between devices, shards(): lax.all_gather(my_rows, 'pipe', axis=0, tiled=True)  31.6 us
    all_to_all x1, blocking collectives, shards(): lax.all_to_all(inverted, 'dp', split_axis=1, concat_axis=0, tiled=True)  29 us
    all_to_all x1, waiting for transfers between devices, shards(): lax.all_to_all(padded, 'dp', split_axis=0, concat_axis=1, tiled=True)  17.8 us
  transfers between devices with their start and end apart: 5, of which 5 were waited for; matrix products, arithmetic and copies ran while one was open for 1% of the time, Pallas kernels for 0%

commit v1 on v0

--- a/solution.py
+++ b/solution.py
@@ -83,7 +83,7 @@
     held_rows = spread_rows[:HOST]
     returned = lax.all_gather(held_rows, "pipe", axis=0, tiled=True)
     own_rows = jnp.einsum("bm,mrc->brc", pick_back, returned, precision=lax.Precision.HIGHEST)
-    inverse = lax.all_gather(own_rows, "dp", axis=1, tiled=True)
+    inverse = jnp.concatenate(lax.all_gather(own_rows, "dp"), axis=1)
     grad_blocks = grad.reshape(nblocks, BLK, grad.shape[1])
     precond = jnp.einsum("brk,bkc->brc", inverse, grad_blocks, precision=lax.Precision.HIGHEST)
     return (precond.reshape(feature_count, grad.shape[1]), held_rows[None])

time: 448 us -> 448 us (level)
  no operation moved by 1% of the time
where the time goes in v1:
time: 448 us; the launch traced here: 447 us
  waiting for transfers between devices  172 us (38%)
  other arithmetic  165 us (37%)
  local copies, waits for them, and re-layouts  39.6 us (9%)
  blocking collectives  29 us (6%)
  matrix products  22.1 us (5%)
  between operations  14.1 us (3%)
  starting transfers between devices  5.2 us (1%)
    another operation x9, other arithmetic, invert_blocks(): cholesky_lower = jnp.linalg.cholesky(shifted)  102 us
    another operation x4, other arithmetic, invert_blocks(): lax.linalg.triangular_solve(cholesky_lower, identity_stack, left_side=Tru...  61.1 us
    reduce_scatter x1, waiting for transfers between devices, shards(): lax.psum_scatter(block_terms.reshape(row_share * lax.axis_size('dp'), nbl...  43.2 us
    all_gather x1, waiting for transfers between devices, shards(): returned = lax.all_gather(held_rows, 'pipe', axis=0, tiled=True)  40.9 us
    all_gather x1, waiting for transfers between devices, shards(): inverse = jnp.concatenate(lax.all_gather(own_rows, 'dp'), axis=1)  38.4 us
    all_gather x1, waiting for transfers between devices, shards(): lax.all_gather(my_rows, 'pipe', axis=0, tiled=True)  31.6 us
    all_to_all x1, blocking collectives, shards(): lax.all_to_all(inverted, 'dp', split_axis=1, concat_axis=0, tiled=True)  29 us
    all_to_all x1, waiting for transfers between devices, shards(): lax.all_to_all(padded, 'dp', split_axis=0, concat_axis=1, tiled=True)  17.9 us
  transfers between devices with their start and end apart: 5, of which 5 were waited for; matrix products, arithmetic and copies ran while one was open for 1% of the time, Pallas kernels for 0%

profile of v1, /device:TPU:0, one launch (start us, length us, event | category | flops | bytes accessed | tf_op | source)
XLA Modules:
  0.0 447.5 jit_solution(5242161687880719674)
XLA Ops:
  7.2 1.7 copy.108
  8.9 2.3 fusion.29
  11.2 3.5 copy.110
  14.8 43.2 %reduce-scatter.2.cloned.1.call-done = f32[32,3072]{1,0:T(8,128)} async-done(((f32[256,3072]{1,0:T(8,128)}), f32[32,3072]{1,0:T(8,128)}) %reduce-scatter.2.cloned.1.call-update) | async-done | bytes 393232 | tf_op jit(solution)/shard_map/reduce_scatter | solution.py:59
  58.4 31.6 %all-gather.5.cloned.1.call-done = f32[128,3072]{1,0:T(8,128)} async-done(((f32[32,3072]{1,0:T(8,128)}), f32[128,3072]{1,0:T(8,128)}) %all-gather.5.cloned.1.call-update) | async-done | bytes 1572880 | tf_op jit(solution)/shard_map/all_gather | solution.py:65
  90.0 1.7 reshape.101
  91.7 0.9 convolution_bitcast_fusion
  92.6 1.1 copy.112
  93.7 4.6 %all-to-all-start = ((f32[24,32,256]{2,1,0:T(8,128)}), f32[24,32,256]{2,1,0:T(8,128)S(1)}, u32[]{:S(2)}, u32[]{:S(2)}) async-start(f32[24,32,256]{2,1,0:T(8,128)} %copy.112), calls=%async_computation.1 | async-start | bytes 1572864 | tf_op jit(solution)/shard_map/all_to_all | solution.py:78
  98.6 0.7 copy.120
  99.5 0.5 iota_multiply_fusion
  100.1 0.6 iota_compare_fusion.2
  100.8 0.6 iota_compare_fusion.1
  101.4 17.9 %all-to-all-done = f32[24,32,256]{2,1,0:T(8,128)S(1)} async-done(((f32[24,32,256]{2,1,0:T(8,128)}), f32[24,32,256]{2,1,0:T(8,128)S(1)}, u32[]{:S(2)}, u32[]{:S(2)}) %all-to-all-start) | async-done | bytes 786464 | tf_op jit(solution)/shard_map/all_to_all | solution.py:78
  119.4 16.4 %copy.114 = f32[3,256,256]{0,2,1:T(8,128)} copy(f32[3,256,256]{2,1,0:T(8,128)S(1)} %bitcast.81) | data formatting | bytes 1572864 | tf_op jit(solution)/shard_map/div | solution.py:78
  135.8 0.3 copy.115
  136.1 2.3 gather_fusion
  138.5 0.6 subtract_add_fusion
  139.1 0.5 copy-done.5
  139.7 0.3 copy.116
  140.0 0.8 fusion.3
  140.8 35.2 %custom-call.16 = f32[3,128,128]{2,1,0:T(8,128)S(1)} custom-call(f32[3,128,128]{2,1,0:T(8,128)S(1)} %cholesky.122), custom_call_target="Cholesky" | custom-call | tf_op jit(solution)/shard_map/jit(cholesky)/cholesky | solution.py:17
  176.1 0.8 select_bitcast_fusion
  176.9 29.5 %custom-call.17 = f32[3,1,128,128]{2,3,1,0:T(8,128)S(1)} custom-call(f32[3,1,128,128]{3,2,1,0:T(8,128)S(1)} %select_bitcast_fusion), custom_call_target="InvertDiagBlocksLowerTriangular" | custom-call | tf_op jit(solution)/shard_map/jit(cholesky)/cholesky | solution.py:17
  206.4 0.4 constant_dynamic-update-slice_fusion.1
  206.7 0.5 convolution_subtract_fusion.1
  207.3 35.4 %custom-call.18 = f32[3,128,128]{2,1,0:T(8,128)S(1)} custom-call(f32[3,128,128]{2,1,0:T(8,128)S(1)} %convolution_subtract_fusion.1), custom_call_target="Cholesky" | custom-call | tf_op jit(solution)/shard_map/jit(cholesky)/cholesky | solution.py:17
  243.1 5.2 %while.1 = (s32[]{:T(128)}, f32[3,256,256]{2,1,0:T(8,128)S(1)}, s32[2,2]{1,0:T(2,128)S(1)}, f32[2,3,128,128]{3,2,0,1:T(8,128)}, s32[]{:T(128)}) while((s32[]{:T(128)}, f32[3,256,256]{2,1,0:T(8,128)S(1)}, s32[2,2]{1,0:T(2,128)S(1)}, f32[2,3,128,128]{3,2,0,1:T(8,128)}, s32[]{:T(128)}) %tuple.29), condition=%wide.while_cond, body=%wide.while_body.sunk | while | flops 2 | bytes 394849 | solution.py:19
  243.2 0.6 fusion.42
  243.7 2.0 bitcast_dynamic-update-slice_fusion.2
  245.7 0.6 fusion.42
  246.3 2.0 bitcast_dynamic-update-slice_fusion.2
  248.3 59.8 %custom-call.19 = f32[3,2,128,128]{2,3,1,0:T(8,128)S(1)} custom-call(f32[3,2,128,128]{3,2,1,0:T(8,128)} %bitcast.90), custom_call_target="InvertDiagBlocksLowerTriangular" | custom-call | tf_op jit(solution)/shard_map/triangular_solve | solution.py:19
  308.1 0.5 fusion.7
  308.6 0.5 convolution_subtract_fusion
  309.1 0.5 fusion.6
  309.7 1.4 convolution_multiply_fusion
  311.1 0.5 copy.125
  311.7 29.0 %all_to_all.27 = f32[3,256,256]{2,0,1:T(4,128)S(1)} all-to-all(f32[3,256,256]{2,0,1:T(4,128)S(1)} %copy.125), channel_id=1, replica_groups=mesh['pipe'=4,'dp'=8] {'dp'}, dimensions={1} | all-to-all | bytes 1572864 | tf_op jit(solution)/shard_map/all_to_all | solution.py:82
  340.9 1.3 copy.128
  342.2 0.3 all-gather.9.cloned.1.call-start
  342.6 0.7 fusion.25
  343.3 40.9 %all-gather.7.cloned.1.call-done = f32[96,32,256]{2,0,1:T(8,128)} async-done(((f32[24,32,256]{2,0,1:T(8,128)}), f32[96,32,256]{2,0,1:T(8,128)}) %all-gather.7.cloned.1.call-update) | async-done | bytes 3145744 | tf_op jit(solution)/shard_map/all_gather | solution.py:84
  384.2 3.0 fusion.20
  387.2 1.0 copy.129
  388.2 38.4 %all-gather.9.cloned.1.call-done = f32[96,32,256]{2,1,0:T(8,128)} async-done(((f32[12,32,256]{2,1,0:T(8,128)}), f32[96,32,256]{2,1,0:T(8,128)}) %all-gather.9.cloned.1.call-update) | async-done | bytes 3145744 | tf_op jit(solution)/shard_map/all_gather | solution.py:86
  426.6 2.3 copy.130
  428.8 12.1 %fusion.30 = f32[12,256,512]{2,1,0:T(8,128)} fusion(f32[12,256,256]{2,1,0:T(8,128)S(1)} %bitcast.80, f32[12,256,512]{2,1,0:T(8,128)} %bitcast.83), kind=kOutput, calls=%fused_computation.65 | convolution fusion | flops 4831838208 | bytes 15728640 | tf_op jit(solution)/shard_map/brk,bkc->brc/dot_general | solution.py:88
  (49 shorter events, 2.1 us)
Async XLA Ops:
  7.2 50.8 %reduce-scatter.2.cloned.1.call-start = ((), (), s32[]{:S(2)}) async-start(), calls=%async_computation.3 | async-start | bytes 3538944 | tf_op jit(solution)/shard_map/reduce_scatter | solution.py:59
  14.7 43.3 %copy-start.3 = (s32[4,12]{1,0:T(4,128)S(1)}, s32[4,12]{1,0:T(4,128)}, u32[]{:S(2)}) copy-start(s32[4,12]{1,0:T(4,128)} %param.5) | copy-start | bytes 580
  14.8 75.2 %all-gather.5.cloned.1.call-start = ((), (), s32[]{:S(2)}) async-start(), calls=%async_computation.4 | async-start | bytes 1966080 | tf_op jit(solution)/shard_map/all_gather | solution.py:65
  58.4 34.2 %copy-start.4 = (s32[4,12]{1,0:T(4,128)}, s32[4,12]{1,0:T(4,128)S(1)}, u32[]{:S(2)}) copy-start(s32[4,12]{1,0:T(4,128)S(1)} %reshape.99) | copy-start | bytes 580
  93.7 25.6 %all-to-all-start = ((f32[24,32,256]{2,1,0:T(8,128)}), f32[24,32,256]{2,1,0:T(8,128)S(1)}, u32[]{:S(2)}, u32[]{:S(2)}) async-start(f32[24,32,256]{2,1,0:T(8,128)} %copy.112), calls=%async_computation.1 | async-start | bytes 1572864 | tf_op jit(solution)/shard_map/all_to_all | solution.py:78
  98.3 285.9 %all-gather.7.cloned.1.call-start = ((), (), s32[]{:S(2)}) async-start(), calls=%async_computation.5 | async-start | bytes 3932160 | tf_op jit(solution)/shard_map/all_gather | solution.py:84
  139.1 0.5 copy-start.5
  140.0 102.9 %copy-start.2 = (pred[256,256]{1,0:T(8,128)(4,1)S(1)}, pred[256,256]{1,0:T(8,128)(4,1)}, u32[]{:S(2)}) copy-start(pred[256,256]{1,0:T(8,128)(4,1)} %iota_compare_fusion.1) | copy-start | bytes 196612
  140.8 102.3 %copy-start.7 = (s32[2]{0:T(128)S(1)}, s32[2]{0:T(128)}, u32[]{:S(2)}) copy-start(s32[2]{0:T(128)} %iota_multiply_fusion) | copy-start | bytes 28
  176.1 132.0 %copy-start.1 = (f32[128,256]{1,0:T(8,128)S(1)}, f32[128,256]{1,0:T(8,128)}, u32[]{:S(2)}) copy-start(f32[128,256]{1,0:T(8,128)} %copy.120) | copy-start | bytes 393220
  242.9 66.8 %copy-start.6 = (f32[3]{0:T(128)S(1)}, f32[3]{0:T(128)}, u32[]{:S(2)}) copy-start(f32[3]{0:T(128)} %get-tuple-element.21) | copy-start | bytes 40
  340.9 47.3 %copy-start = (f32[8,3,32,256]{3,2,1,0:T(8,128)}, f32[8,3,32,256]{3,2,1,0:T(8,128)S(1)}, u32[]{:S(2)}) copy-start(f32[8,3,32,256]{3,2,1,0:T(8,128)S(1)} %copy.127) | copy-start | bytes 2359300
  342.2 84.3 %all-gather.9.cloned.1.call-start = ((), (), s32[]{:S(2)}) async-start(), calls=%async_computation.6 | async-start | bytes 3538944 | tf_op jit(solution)/shard_map/all_gather | solution.py:86
Sparse Core Ops, SparseCore 0:
  14.9 43.0 reduce-scatter.1
  59.8 30.0 all-gather.4
  342.4 41.7 all-gather.6
  388.3 38.2 all-gather.8
